TPU v7x, 32 devices: a whole 2x2x4 slice. The times are simulated.
32 devices in a mesh: pipe: 4 (over y, core), tensor: 8 (over z, x).
Axes of the slice: x: 2, y: 2, z: 4, core: 2. Of those that a mesh axis runs over, the one named last changes fastest.
Arguments:
- patches: bfloat16 [16384, 1280], P(('pipe', 'tensor')), may hold values from -6 to 6
- attn_gain: float32 [1280], replicated, may hold values from 0.25 to 1.75
- w_qkv: bfloat16 [1280, 3840], P('tensor', 'pipe'), may hold values from -0.1118034 to 0.1118034
- w_out: bfloat16 [1280, 1280], P('tensor', 'pipe'), may hold values from -0.15625 to 0.15625
- merge_gain: float32 [1280], replicated, may hold values from 0.25 to 1.75
- window_ids: int32 [16384], P(('pipe', 'tensor')), may hold values from 0 to 127, as said below
- image_patches: int32 [128], P(('pipe', 'tensor')), may hold values from 0 to 512, as said below
- image_sample: int32 [128], P(('pipe', 'tensor')), may hold values from 0 to 7
Outputs:
- vision_seq: bfloat16 [4, 128, 8, 5120], P('pipe', None, 'tensor')
Inputs may be any that keep to these rules, and one draw needn't show every extreme that they name: `window_ids`: Non-decreasing within each bundle and equal over each 4 consecutive slots; every window lies within one aligned block of 64 slots of a bundle. `image_patches`: multiples of 128; the images of one bundle take at most 512 slots and at least half of them, and in every micro-batch some bundle is full.
All inputs are finite; a program needn't handle non-finite values.
Results may differ from a plain program's by a relative error of at most 0.0053.
Values may be sent and summed in bfloat16 or wider, within the bound.
A program may use at most 64 MiB of HBM per device.

v0:
```python
import math
import jax
import jax.numpy as jnp
from jax import lax
from jax.sharding import PartitionSpec as P

HEADS = 16
WINDOW = 64
SAMPLES = 8
epsilon = 1e-06


def normalize(values, gain_row):
    return (
        values * lax.rsqrt(jnp.mean(values * values, axis=-1, keepdims=True) + epsilon) * gain_row
    )


def token_positions(starts, merged_count, token_count):
    offsets = jnp.cumsum(merged_count) - merged_count
    token_index = jnp.arange(token_count, dtype=jnp.int32)
    inside = (token_index[None, :] >= offsets[:, None]) & (
        token_index[None, :] < (offsets + merged_count)[:, None]
    )
    position = jnp.sum(
        jnp.where(inside, starts[:, None] + token_index[None, :] - offsets[:, None], 0), axis=0
    )
    return jnp.where(jnp.any(inside, axis=0), position, -1)


def body(patches, attn_gain, w_qkv, w_out, merge_gain, window_ids, image_patches, image_sample):
    patch_count, feature_width = patches.shape
    token_count = patch_count // 4
    group_size = lax.axis_size("tensor")
    own_index = lax.axis_index("tensor")
    residual = patches.astype(jnp.float32)
    normed = normalize(residual, attn_gain).astype(jnp.bfloat16)
    qkv_rows = lax.all_gather(w_qkv, "tensor", axis=0, tiled=True)
    qkv = jnp.dot(
        normed,
        lax.all_gather(qkv_rows, "pipe", axis=1, tiled=True),
        preferred_element_type=jnp.float32,
    ).astype(jnp.bfloat16)
    head_width = feature_width // HEADS
    tile_count = patch_count // WINDOW

    def split_heads(block):
        return block.reshape(tile_count, WINDOW, HEADS, head_width)

    queries = split_heads(qkv[:, :feature_width])
    keys_tile = split_heads(qkv[:, feature_width : 2 * feature_width])
    values_tile = split_heads(qkv[:, 2 * feature_width :])
    scores = jnp.einsum(
        "tqhd,tkhd->thqk", queries, keys_tile, preferred_element_type=jnp.float32
    ) * (1.0 / math.sqrt(head_width))
    live_row = jnp.arange(patch_count, dtype=jnp.int32) < jnp.sum(image_patches)
    window_tile = window_ids.reshape(tile_count, WINDOW)
    live_tile = live_row.reshape(tile_count, WINDOW)
    allowed = (window_tile[:, :, None] == window_tile[:, None, :]) & live_tile[:, None, :]
    scores = jnp.where(allowed[:, None, :, :], scores, -1e30)
    row_max = jnp.max(scores, axis=-1, keepdims=True)
    exponent = jnp.exp(scores - row_max)
    weights = (exponent / jnp.sum(exponent, axis=-1, keepdims=True)).astype(jnp.bfloat16)
    context = jnp.einsum(
        "thqk,tkhd->tqhd", weights, values_tile, preferred_element_type=jnp.float32
    ).reshape(patch_count, feature_width)
    context = jnp.where(live_row[:, None], context, 0.0).astype(jnp.bfloat16)
    proj_rows = lax.all_gather(w_out, "tensor", axis=0, tiled=True)
    attended = jnp.dot(
        context,
        lax.all_gather(proj_rows, "pipe", axis=1, tiled=True),
        preferred_element_type=jnp.float32,
    )
    hidden = residual + attended
    merged = (
        normalize(hidden, merge_gain).astype(jnp.bfloat16).reshape(token_count, 4 * feature_width)
    )
    outgoing = merged.reshape(token_count // group_size, group_size, 4 * feature_width)
    merged_count = image_patches // 4
    sample_hot = image_sample[:, None] == jnp.arange(SAMPLES, dtype=jnp.int32)[None, :]
    sample_tally = jnp.sum(jnp.where(sample_hot, merged_count[:, None], 0), axis=0)
    all_tallies = lax.all_gather(sample_tally[None, :], "tensor", axis=0, tiled=True)
    source_ranks = jnp.arange(group_size, dtype=jnp.int32)
    before = jnp.sum(jnp.where((source_ranks < own_index)[:, None], all_tallies, 0), axis=0)
    totals = jnp.sum(all_tallies, axis=0)
    sample_index = jnp.arange(SAMPLES, dtype=jnp.int32)
    sample_base = jnp.sum(
        jnp.where(sample_index[None, :] < sample_index[:, None], totals[None, :], 0), axis=1
    )
    image_order = jnp.arange(image_sample.shape[0], dtype=jnp.int32)
    same_before = (image_sample[None, :] == image_sample[:, None]) & (
        image_order[None, :] < image_order[:, None]
    )
    earlier = jnp.sum(jnp.where(same_before, merged_count[None, :], 0), axis=1)
    starts = jnp.sum(jnp.where(sample_hot, (sample_base + before)[None, :], 0), axis=1) + earlier
    position = token_positions(starts, merged_count, token_count)
    outgoing_position = position.reshape(token_count // group_size, group_size)
    received, received_position = (
        lax.all_to_all(outgoing, "tensor", split_axis=1, concat_axis=0, tiled=True),
        lax.all_to_all(outgoing_position, "tensor", split_axis=1, concat_axis=0, tiled=True),
    )
    dest_rows = received_position.reshape(token_count) // group_size
    placement = (jnp.arange(token_count, dtype=jnp.int32)[:, None] == dest_rows[None, :]).astype(
        jnp.bfloat16
    )
    placed = jnp.dot(
        placement,
        received.reshape(token_count, 4 * feature_width),
        preferred_element_type=jnp.float32,
    )
    return placed.astype(jnp.bfloat16).reshape(1, token_count, 1, 4 * feature_width)


def solution(mesh):
    return jax.shard_map(
        body,
        mesh=mesh,
        in_specs=(
            P(("pipe", "tensor"), None),
            P(),
            P("tensor", "pipe"),
            P("tensor", "pipe"),
            P(),
            P(("pipe", "tensor")),
            P(("pipe", "tensor")),
            P(("pipe", "tensor")),
        ),
        out_specs=P("pipe", None, "tensor", None),
        check_vma=False,
    )
```

profile of v0, /device:TPU:0, one launch (start us, length us, event | category | flops | bytes accessed | tf_op | source)
XLA Modules:
  0.0 223.8 jit_solution(180956799762831658)
XLA Ops:
  6.5 0.7 all-gather.5.cloned.1.call-update
  7.3 59.4 %all-gather.5.cloned.1.call-done = bf16[1280,960]{1,0:T(8,128)(2,1)} async-done(((bf16[160,960]{1,0:T(8,128)(2,1)}), bf16[1280,960]{1,0:T(8,128)(2,1)}) %all-gather.5.cloned.1.call-update) | async-done | bytes 2457616 | tf_op jit(solution)/shard_map/all_gather | solution.py:38
  66.7 4.4 %copy.40 = bf16[1280,960]{0,1:T(8,128)(2,1)} copy(bf16[1280,960]{1,0:T(8,128)(2,1)} %all-gather.5.cloned.1.call-done) | data formatting | bytes 4915200 | tf_op jit(solution)/shard_map/all_gather | solution.py:38
  71.2 33.0 %all_gather.18 = bf16[1280,320]{1,0:T(8,128)(2,1)S(1)} all-gather(bf16[160,320]{1,0:T(8,128)(2,1)S(1)} %copy-done.3), channel_id=1, replica_groups=mesh['pipe'=4,'tensor'=8] {'tensor'}, dimensions={0}, use_global_device_ids=true | all-gather | bytes 921600 | tf_op jit(solution)/shard_map/all_gather | solution.py:68
  104.2 1.3 copy.46
  105.5 0.6 and_select_fusion.1
  106.4 0.6 dynamic-slice
  107.7 0.2 dynamic-update-slice
  108.0 8.6 %all-reduce = s32[64]{0:T(128)S(1)} all-reduce(s32[64]{0:T(128)S(1)} %dynamic-update-slice), channel_id=2, replica_groups=mesh['pipe'=4,'tensor'=8] {'tensor'}, use_global_device_ids=true, to_apply=%add | all-reduce | flops 64 | bytes 512
  117.5 0.7 copy.39
  118.2 4.5 %all-to-all-start = ((s32[16,8,1]{0,2,1:T(1,128)}), s32[16,8,1]{0,2,1:T(1,128)S(1)}, u32[]{:S(2)}, u32[]{:S(2)}) async-start(s32[16,8,1]{0,2,1:T(1,128)} %copy.39), calls=%async_computation | async-start | bytes 8192 | tf_op jit(solution)/shard_map/all_to_all | solution.py:100
  122.8 0.6 iota_compare_fusion.3
  123.5 0.7 add_compare_fusion
  124.1 0.3 fusion.3
  124.7 11.6 %all-gather.7.cloned.1.call-done = bf16[1280,3840]{0,1:T(8,128)(2,1)} async-done(((bf16[1280,960]{0,1:T(8,128)(2,1)}), bf16[1280,3840]{0,1:T(8,128)(2,1)}) %all-gather.7.cloned.1.call-update) | async-done | bytes 9830416 | tf_op jit(solution)/shard_map/all_gather | solution.py:41
  136.3 9.5 %convolution_convert_fusion.1 = bf16[512,3840]{1,0:T(8,128)(2,1)S(1)} fusion(bf16[1280,3840]{0,1:T(8,128)(2,1)} %all-gather.7.cloned.1.call-done, bf16[512,1280]{1,0:T(8,128)(2,1)S(1)} %copy-done.1, f32[1280]{0:T(1024)S(1)} %copy-done.7, f32[512]{0:T(512)S(1)} %add_rsqrt_fusion.1), kind=kOutput, calls=%fused_computation.2 | convolution fusion | flops 5037752320 | bytes 15080448 | tf_op jit(solution)/shard_map/dot_general | solution.py:39
  145.8 1.7 fusion.26
  147.5 4.1 %reshape.158 = bf16[8,64,16,80]{3,2,1,0:T(8,128)(2,1)S(1)} reshape(bf16[512,1280]{1,0:T(8,128)(2,1)} %get-tuple-element.9) | data formatting | bytes 2621440 | tf_op jit(solution)/shard_map/reshape | solution.py:48
  151.6 5.0 %reshape.159 = bf16[8,64,16,80]{3,2,1,0:T(8,128)(2,1)} reshape(bf16[512,1280]{1,0:T(8,128)(2,1)} %get-tuple-element.8) | data formatting | bytes 2621440 | tf_op jit(solution)/shard_map/reshape | solution.py:48
  156.7 4.1 %reshape.157 = bf16[8,64,16,80]{3,2,1,0:T(8,128)(2,1)} reshape(bf16[512,1280]{1,0:T(8,128)(2,1)S(1)} %get-tuple-element.7) | data formatting | bytes 2621440 | tf_op jit(solution)/shard_map/reshape | solution.py:48
  160.8 2.8 %fusion.7 = f32[8,16,64,64]{2,3,1,0:T(8,128)S(1)} fusion(bf16[8,64,16,80]{3,2,1,0:T(8,128)(2,1)} %reshape.159, bf16[8,64,16,80]{3,2,1,0:T(8,128)(2,1)S(1)} %reshape.158), kind=kOutput, calls=%fused_computation.19 | convolution fusion | flops 83886080 | bytes 4718592 | tf_op jit(solution)/shard_map/tqhd,tkhd->thqk/dot_general | solution.py:53
  163.6 1.5 fusion.27
  165.2 1.2 convolution_bitcast_fusion
  166.4 1.4 copy.45
  167.8 3.3 %reshape.160 = bf16[512,1280]{1,0:T(8,128)(2,1)} reshape(bf16[8,64,16,80]{3,2,1,0:T(8,128)(2,1)S(1)} %copy.45) | data formatting | bytes 2621440 | tf_op jit(solution)/shard_map/reshape | solution.py:66
  171.1 4.3 %multiply_reduce_fusion = (f32[512]{0:T(512)S(1)}, f32[512,1280]{1,0:T(8,128)S(1)}) fusion(bf16[1280,1280]{0,1:T(8,128)(2,1)} %all-gather.9.cloned.1.call-done, bf16[512,1280]{1,0:T(8,128)(2,1)} %reshape.160, pred[512]{0:T(512)(128)(4,1)S(1)} %iota_compare_fusion.3, bf16[512,1280]{1,0:T(8,128)(2,1)S(1)} %copy-done.2), kind=kOutput, calls=%fused_computation.15 | convolution fusion | flops 1680997888 | bytes 8522240 | tf_op jit(solution)/shard_map/dot_general | solution.py:69
  175.4 0.3 multiply_convert_fusion
  175.7 0.8 reshape_reshape.3
  176.6 1.8 copy.47
  178.3 5.5 %all-to-all-start.1 = ((bf16[16,8,5120]{2,0,1:T(8,128)(2,1)}), bf16[16,8,5120]{2,0,1:T(8,128)(2,1)S(1)}, u32[]{:S(2)}, u32[]{:S(2)}) async-start(bf16[16,8,5120]{2,0,1:T(8,128)(2,1)} %copy.47), calls=%async_computation.1 | async-start | bytes 2621440 | tf_op jit(solution)/shard_map/all_to_all | solution.py:99
  184.0 31.7 %all-to-all-done.1 = bf16[16,8,5120]{2,0,1:T(8,128)(2,1)S(1)} async-done(((bf16[16,8,5120]{2,0,1:T(8,128)(2,1)}), bf16[16,8,5120]{2,0,1:T(8,128)(2,1)S(1)}, u32[]{:S(2)}, u32[]{:S(2)}) %all-to-all-start.1) | async-done | bytes 1310752 | tf_op jit(solution)/shard_map/all_to_all | solution.py:99
  215.7 1.6 fusion.1
  (50 shorter events, 1.9 us)
Async XLA Ops:
  6.5 60.1 %all-gather.5.cloned.1.call-start = ((), (), s32[]{:S(2)}) async-start(), calls=%async_computation.2 | async-start | bytes 2949120 | tf_op jit(solution)/shard_map/all_gather | solution.py:38
  7.3 63.9 %copy-start.3 = (bf16[160,320]{1,0:T(8,128)(2,1)S(1)}, bf16[160,320]{1,0:T(8,128)(2,1)}, u32[]{:S(2)}) copy-start(bf16[160,320]{1,0:T(8,128)(2,1)} %param.11) | copy-start | bytes 307204
  7.3 129.0 %all-gather.7.cloned.1.call-start = ((), (), s32[]{:S(2)}) async-start(), calls=%async_computation.3 | async-start | bytes 12288000 | tf_op jit(solution)/shard_map/all_gather | solution.py:41
  71.0 34.4 %copy-start.8 = (s32[4]{0:T(128)S(1)}, s32[4]{0:T(128)}, u32[]{:S(2)}) copy-start(s32[4]{0:T(128)} %param.14) | copy-start | bytes 52
  71.0 35.1 %copy-start.6 = (s32[4]{0:T(128)S(1)}, s32[4]{0:T(128)}, u32[]{:S(2)}) copy-start(s32[4]{0:T(128)} %param.15) | copy-start | bytes 52
  71.0 35.4 %copy-start.9 = (u32[32]{0:T(128)S(1)}, u32[32]{0:T(128)}, u32[]{:S(2)}) copy-start(u32[32]{0:T(128)} %constant.61) | copy-start | bytes 388
  71.1 51.7 %copy-start.5 = (s32[512]{0:T(512)S(1)}, s32[512]{0:T(512)}, u32[]{:S(2)}) copy-start(s32[512]{0:T(512)} %param.13) | copy-start | bytes 6148
  71.1 53.1 %copy-start.1 = (bf16[512,1280]{1,0:T(8,128)(2,1)S(1)}, bf16[512,1280]{1,0:T(8,128)(2,1)}, u32[]{:S(2)}) copy-start(bf16[512,1280]{1,0:T(8,128)(2,1)} %param.8) | copy-start | bytes 3932164
  71.1 65.2 %copy-start.7 = (f32[1280]{0:T(1024)S(1)}, f32[1280]{0:T(1024)}, u32[]{:S(2)}) copy-start(f32[1280]{0:T(1024)} %param.9) | copy-start | bytes 15364
  71.1 99.9 %all-gather.9.cloned.1.call-start = ((), (), s32[]{:S(2)}) async-start(), calls=%async_computation.4 | async-start | bytes 4096000 | tf_op jit(solution)/shard_map/all_gather | solution.py:71
  118.2 60.2 %all-to-all-start = ((s32[16,8,1]{0,2,1:T(1,128)}), s32[16,8,1]{0,2,1:T(1,128)S(1)}, u32[]{:S(2)}, u32[]{:S(2)}) async-start(s32[16,8,1]{0,2,1:T(1,128)} %copy.39), calls=%async_computation | async-start | bytes 8192 | tf_op jit(solution)/shard_map/all_to_all | solution.py:100
  163.6 1.6 copy-start
  167.8 3.3 %copy-start.2 = (bf16[512,1280]{1,0:T(8,128)(2,1)S(1)}, bf16[512,1280]{1,0:T(8,128)(2,1)}, u32[]{:S(2)}) copy-start(bf16[512,1280]{1,0:T(8,128)(2,1)} %param.8) | copy-start | bytes 3932164
  171.1 4.4 %copy-start.4 = (f32[1280]{0:T(1024)S(1)}, f32[1280]{0:T(1024)}, u32[]{:S(2)}) copy-start(f32[1280]{0:T(1024)} %param.12) | copy-start | bytes 15364
  178.3 37.3 %all-to-all-start.1 = ((bf16[16,8,5120]{2,0,1:T(8,128)(2,1)}), bf16[16,8,5120]{2,0,1:T(8,128)(2,1)S(1)}, u32[]{:S(2)}, u32[]{:S(2)}) async-start(bf16[16,8,5120]{2,0,1:T(8,128)(2,1)} %copy.47), calls=%async_computation.1 | async-start | bytes 2621440 | tf_op jit(solution)/shard_map/all_to_all | solution.py:99
Sparse Core Ops, SparseCore 0:
  9.5 57.1 all-gather.4
  71.2 65.0 all-gather.6
  137.8 29.2 all-gather.8
where the time goes:
time: 224 us
  waiting for transfers between devices  103 us (46%)
  blocking collectives  41.6 us (19%)
  local copies, waits for them, and re-layouts  29.9 us (13%)
  matrix products  19.4 us (9%)
  between operations  14 us (6%)
  starting transfers between devices  10.1 us (5%)
  other arithmetic  5.32 us (2%)
    all_gather x1, waiting for transfers between devices, body(): qkv_rows = lax.all_gather(w_qkv, 'tensor', axis=0, tiled=True)  59.4 us
    all_gather x1, blocking collectives, body(): proj_rows = lax.all_gather(w_out, 'tensor', axis=0, tiled=True)  33 us
    all_to_all x1, waiting for transfers between devices, body(): lax.all_to_all(outgoing, 'tensor', split_axis=1, concat_axis=0, tiled=True)  31.7 us
    reshape x3, local copies, waits for them, and re-layouts, split_heads(): return block.reshape(tile_count, WINDOW, HEADS, head_width)  13.2 us
    all_gather x1, waiting for transfers between devices, body(): lax.all_gather(qkv_rows, 'pipe', axis=1, tiled=True)  11.6 us
    dot_general x1, matrix products, body(): jnp.dot(normed, lax.all_gather(qkv_rows, 'pipe', axis=1, tiled=True), pre...  9.49 us
    unnamed x1, blocking collectives  8.57 us
    all_to_all x1, starting transfers between devices, body(): lax.all_to_all(outgoing, 'tensor', split_axis=1, concat_axis=0, tiled=True)  5.51 us
  transfers between devices with their start and end apart: 5, of which 3 were waited for; matrix products, arithmetic and copies ran while one was open for 22% of the time, Pallas kernels for 0%

commit v1 on v0

--- a/solution.py
+++ b/solution.py
@@ -68,7 +68,12 @@
     proj_rows = lax.all_gather(w_out, "tensor", axis=0, tiled=True)
     attended = jnp.dot(
         context,
-        lax.all_gather(proj_rows, "pipe", axis=1, tiled=True),
+        jnp.concatenate(
+            jax.lax.all_to_all(
+                jnp.stack(jax.lax.axis_size("pipe") * [proj_rows], axis=0), "pipe", 0, 0
+            ),
+            axis=1,
+        ),
         preferred_element_type=jnp.float32,
     )
     hidden = residual + attended

time: 224 us -> 254 us (1.13)
  waiting for transfers between devices: 103 us -> 122 us
  starting transfers between devices: 10.1 us -> 19.7 us
    all_gather x1, waiting for transfers between devices: 11.6 us -> 31.2 us  [body(): lax.all_gather(qkv_rows, 'pipe', axis=1, tiled=True)]
    all_to_all x0 -> x1, starting transfers between devices: none -> 4.81 us  [body(): jax.lax.all_to_all(jnp.stack(jax.lax.axis_size('pipe') * [proj_rows], axi...]
    convert_element_type x0 -> x2, local copies, waits for them, and re-layouts: none -> 4.64 us  [body(): context = jnp.where(live_row[:, None], context, 0.0).astype(jnp.bfloat16)]
    all_to_all x1, starting transfers between devices: 4.54 us -> 8.89 us  [body(): lax.all_to_all(outgoing_position, 'tensor', split_axis=1, concat_axis=0,...]
    reshape x1 -> x0, local copies, waits for them, and re-layouts: 3.27 us -> none  [body(): context = jnp.einsum('thqk,tkhd->tqhd', weights, values_tile, preferred_e...]
  transfers between devices with their start and end apart: 5 -> 5, of which waited for: 3 -> 3; matrix products, arithmetic and copies ran while one was open for 22% -> 19% of each run, Pallas kernels for 0% -> 0%
where the time goes in v1:
time: 254 us; the launch traced here: 253 us
  waiting for transfers between devices  122 us (48%)
  blocking collectives  41.4 us (16%)
  local copies, waits for them, and re-layouts  31 us (12%)
  starting transfers between devices  19.7 us (8%)
  matrix products  19.6 us (8%)
  between operations  14.2 us (6%)
  other arithmetic  4.66 us (2%)
    all_gather x1, waiting for transfers between devices, body(): qkv_rows = lax.all_gather(w_qkv, 'tensor', axis=0, tiled=True)  59.4 us
    all_gather x1, blocking collectives, body(): proj_rows = lax.all_gather(w_out, 'tensor', axis=0, tiled=True)  32.9 us
    all_gather x1, waiting for transfers between devices, body(): lax.all_gather(qkv_rows, 'pipe', axis=1, tiled=True)  31.2 us
    all_to_all x1, waiting for transfers between devices, body(): lax.all_to_all(outgoing, 'tensor', split_axis=1, concat_axis=0, tiled=True)  31.1 us
    reshape x3, local copies, waits for them, and re-layouts, split_heads(): return block.reshape(tile_count, WINDOW, HEADS, head_width)  13.2 us
    dot_general x1, matrix products, body(): jnp.dot(normed, lax.all_gather(qkv_rows, 'pipe', axis=1, tiled=True), pre...  9.49 us
    all_to_all x1, starting transfers between devices, body(): lax.all_to_all(outgoing_position, 'tensor', split_axis=1, concat_axis=0,...  8.89 us
    unnamed x1, blocking collectives  8.57 us
  transfers between devices with their start and end apart: 5, of which 3 were waited for; matrix products, arithmetic and copies ran while one was open for 19% of the time, Pallas kernels for 0%

profile of v1, /device:TPU:0, one launch (start us, length us, event | category | flops | bytes accessed | tf_op | source)
XLA Modules:
  0.0 253.1 jit_solution(16371545309001737180)
XLA Ops:
  6.5 0.7 all-gather.4.cloned.1.call-update
  7.3 59.4 %all-gather.4.cloned.1.call-done = bf16[1280,960]{1,0:T(8,128)(2,1)} async-done(((bf16[160,960]{1,0:T(8,128)(2,1)}), bf16[1280,960]{1,0:T(8,128)(2,1)}) %all-gather.4.cloned.1.call-update) | async-done | bytes 2457616 | tf_op jit(solution)/shard_map/all_gather | solution.py:38
  66.7 4.4 %copy.41 = bf16[1280,960]{0,1:T(8,128)(2,1)} copy(bf16[1280,960]{1,0:T(8,128)(2,1)} %all-gather.4.cloned.1.call-done) | data formatting | bytes 4915200 | tf_op jit(solution)/shard_map/all_gather | solution.py:38
  71.1 32.9 %all_gather.15 = bf16[1280,320]{1,0:T(8,128)(2,1)S(1)} all-gather(bf16[160,320]{1,0:T(8,128)(2,1)S(1)} %copy-done.3), channel_id=1, replica_groups=mesh['pipe'=4,'tensor'=8] {'tensor'}, dimensions={0}, use_global_device_ids=true | all-gather | bytes 921600 | tf_op jit(solution)/shard_map/all_gather | solution.py:68
  103.9 0.6 copy.47
  104.5 1.9 stack.2
  106.4 4.8 %all-to-all-start.1 = ((bf16[4,1280,320]{1,2,0:T(8,128)(2,1)}), bf16[4,1280,320]{1,2,0:T(8,128)(2,1)}, u32[]{:S(2)}, u32[]{:S(2)}) async-start(bf16[4,1280,320]{1,2,0:T(8,128)(2,1)} %stack.2), calls=%async_computation.1 | async-start | bytes 6553600 | tf_op jit(solution)/shard_map/all_to_all | solution.py:72
  111.4 0.6 and_select_fusion.1
  112.2 0.6 dynamic-slice
  113.6 8.6 %all-reduce = s32[64]{0:T(128)S(1)} all-reduce(s32[64]{0:T(128)S(1)} %dynamic-update-slice), channel_id=2, replica_groups=mesh['pipe'=4,'tensor'=8] {'tensor'}, use_global_device_ids=true, to_apply=%add | all-reduce | flops 64 | bytes 512
  123.2 0.7 copy.40
  123.8 0.7 add_compare_fusion
  124.5 0.3 fusion.3
  125.1 31.2 %all-gather.6.cloned.1.call-done = bf16[1280,3840]{0,1:T(8,128)(2,1)} async-done(((bf16[1280,960]{0,1:T(8,128)(2,1)}), bf16[1280,3840]{0,1:T(8,128)(2,1)}) %all-gather.6.cloned.1.call-update) | async-done | bytes 9830416 | tf_op jit(solution)/shard_map/all_gather | solution.py:41
  156.3 9.5 %convolution_convert_fusion.1 = bf16[512,3840]{1,0:T(8,128)(2,1)S(1)} fusion(bf16[1280,3840]{0,1:T(8,128)(2,1)} %all-gather.6.cloned.1.call-done, bf16[512,1280]{1,0:T(8,128)(2,1)S(1)} %copy-done.1, f32[1280]{0:T(1024)S(1)} %copy-done.7, f32[512]{0:T(512)S(1)} %add_rsqrt_fusion.1), kind=kOutput, calls=%fused_computation.2 | convolution fusion | flops 5037752320 | bytes 15080448 | tf_op jit(solution)/shard_map/dot_general | solution.py:39
  165.8 1.7 fusion.26
  167.5 4.1 %reshape.171 = bf16[8,64,16,80]{3,2,1,0:T(8,128)(2,1)S(1)} reshape(bf16[512,1280]{1,0:T(8,128)(2,1)} %get-tuple-element.8) | data formatting | bytes 2621440 | tf_op jit(solution)/shard_map/reshape | solution.py:48
  171.6 5.0 %reshape.170 = bf16[8,64,16,80]{3,2,1,0:T(8,128)(2,1)} reshape(bf16[512,1280]{1,0:T(8,128)(2,1)} %get-tuple-element.9) | data formatting | bytes 2621440 | tf_op jit(solution)/shard_map/reshape | solution.py:48
  176.7 4.1 %reshape.169 = bf16[8,64,16,80]{3,2,1,0:T(8,128)(2,1)} reshape(bf16[512,1280]{1,0:T(8,128)(2,1)S(1)} %get-tuple-element.7) | data formatting | bytes 2621440 | tf_op jit(solution)/shard_map/reshape | solution.py:48
  180.7 2.8 %fusion.7 = f32[8,16,64,64]{2,3,1,0:T(8,128)S(1)} fusion(bf16[8,64,16,80]{3,2,1,0:T(8,128)(2,1)S(1)} %reshape.171, bf16[8,64,16,80]{3,2,1,0:T(8,128)(2,1)} %reshape.170), kind=kOutput, calls=%fused_computation.18 | convolution fusion | flops 83886080 | bytes 4718592 | tf_op jit(solution)/shard_map/tqhd,tkhd->thqk/dot_general | solution.py:53
  183.6 1.5 fusion.27
  185.2 1.4 fusion.14
  186.6 1.4 copy.46
  188.0 3.3 %convert_element_type.34 = bf16[512,1280]{1,0:T(8,128)(2,1)} reshape(bf16[8,64,16,80]{3,2,1,0:T(8,128)(2,1)S(1)} %copy.46) | data formatting | bytes 2621440 | tf_op jit(solution)/shard_map/convert_element_type | solution.py:67
  191.3 8.9 %all-to-all-start = ((s32[16,8,1]{0,2,1:T(1,128)}), s32[16,8,1]{0,2,1:T(1,128)S(1)}, u32[]{:S(2)}, u32[]{:S(2)}) async-start(s32[16,8,1]{0,2,1:T(1,128)} %copy.40), calls=%async_computation | async-start | bytes 8192 | tf_op jit(solution)/shard_map/all_to_all | solution.py:105
  200.2 4.4 %multiply_reduce_fusion = (f32[512]{0:T(512)S(1)}, f32[512,1280]{1,0:T(8,128)S(1)}) fusion(bf16[512,1280]{1,0:T(8,128)(2,1)} %convert_element_type.34, bf16[1280,1280]{0,1:T(8,128)(2,1)} %bitcast.6, bf16[512,1280]{1,0:T(8,128)(2,1)S(1)} %copy-done.2), kind=kOutput, calls=%fused_computation.16 | convolution fusion | flops 1680342528 | bytes 8521728 | tf_op jit(solution)/shard_map/dot_general | solution.py:69
  204.5 0.3 multiply_convert_fusion
  204.8 0.8 reshape_reshape.3
  205.7 1.8 copy.48
  207.5 6.0 %all-to-all-start.2 = ((bf16[16,8,5120]{2,0,1:T(8,128)(2,1)}), bf16[16,8,5120]{2,0,1:T(8,128)(2,1)S(1)}, u32[]{:S(2)}, u32[]{:S(2)}) async-start(bf16[16,8,5120]{2,0,1:T(8,128)(2,1)} %copy.48), calls=%async_computation.2 | async-start | bytes 2621440 | tf_op jit(solution)/shard_map/all_to_all | solution.py:104
  213.6 31.1 %all-to-all-done.2 = bf16[16,8,5120]{2,0,1:T(8,128)(2,1)S(1)} async-done(((bf16[16,8,5120]{2,0,1:T(8,128)(2,1)}), bf16[16,8,5120]{2,0,1:T(8,128)(2,1)S(1)}, u32[]{:S(2)}, u32[]{:S(2)}) %all-to-all-start.2) | async-done | bytes 1310752 | tf_op jit(solution)/shard_map/all_to_all | solution.py:104
  244.7 1.6 fusion.1
  (49 shorter events, 2.0 us)
Async XLA Ops:
  6.5 60.1 %all-gather.4.cloned.1.call-start = ((), (), s32[]{:S(2)}) async-start(), calls=%async_computation.3 | async-start | bytes 2949120 | tf_op jit(solution)/shard_map/all_gather | solution.py:38
  7.3 63.8 %copy-start.3 = (bf16[160,320]{1,0:T(8,128)(2,1)S(1)}, bf16[160,320]{1,0:T(8,128)(2,1)}, u32[]{:S(2)}) copy-start(bf16[160,320]{1,0:T(8,128)(2,1)} %param.11) | copy-start | bytes 307204
  7.3 149.0 %all-gather.6.cloned.1.call-start = ((), (), s32[]{:S(2)}) async-start(), calls=%async_computation.4 | async-start | bytes 12288000 | tf_op jit(solution)/shard_map/all_gather | solution.py:41
  106.4 4.9 %copy-start.5 = (s32[512]{0:T(512)S(1)}, s32[512]{0:T(512)}, u32[]{:S(2)}) copy-start(s32[512]{0:T(512)} %param.13) | copy-start | bytes 6148
  106.4 4.9 %copy-start.8 = (s32[4]{0:T(128)S(1)}, s32[4]{0:T(128)}, u32[]{:S(2)}) copy-start(s32[4]{0:T(128)} %param.14) | copy-start | bytes 52
  106.4 5.8 %copy-start.9 = (u32[32]{0:T(128)S(1)}, u32[32]{0:T(128)}, u32[]{:S(2)}) copy-start(u32[32]{0:T(128)} %constant.62) | copy-start | bytes 388
  106.4 6.9 %copy-start.6 = (s32[4]{0:T(128)S(1)}, s32[4]{0:T(128)}, u32[]{:S(2)}) copy-start(s32[4]{0:T(128)} %param.15) | copy-start | bytes 52
  106.4 18.1 %copy-start.1 = (bf16[512,1280]{1,0:T(8,128)(2,1)S(1)}, bf16[512,1280]{1,0:T(8,128)(2,1)}, u32[]{:S(2)}) copy-start(bf16[512,1280]{1,0:T(8,128)(2,1)} %param.8) | copy-start | bytes 3932164
  106.4 49.8 %copy-start.7 = (f32[1280]{0:T(1024)S(1)}, f32[1280]{0:T(1024)}, u32[]{:S(2)}) copy-start(f32[1280]{0:T(1024)} %param.9) | copy-start | bytes 15364
  106.4 84.8 %all-to-all-start.1 = ((bf16[4,1280,320]{1,2,0:T(8,128)(2,1)}), bf16[4,1280,320]{1,2,0:T(8,128)(2,1)}, u32[]{:S(2)}, u32[]{:S(2)}) async-start(bf16[4,1280,320]{1,2,0:T(8,128)(2,1)} %stack.2), calls=%async_computation.1 | async-start | bytes 6553600 | tf_op jit(solution)/shard_map/all_to_all | solution.py:72
  183.6 1.6 copy-start
  188.0 12.2 %copy-start.2 = (bf16[512,1280]{1,0:T(8,128)(2,1)S(1)}, bf16[512,1280]{1,0:T(8,128)(2,1)}, u32[]{:S(2)}) copy-start(bf16[512,1280]{1,0:T(8,128)(2,1)} %param.8) | copy-start | bytes 3932164
  191.3 16.2 %all-to-all-start = ((s32[16,8,1]{0,2,1:T(1,128)}), s32[16,8,1]{0,2,1:T(1,128)S(1)}, u32[]{:S(2)}, u32[]{:S(2)}) async-start(s32[16,8,1]{0,2,1:T(1,128)} %copy.40), calls=%async_computation | async-start | bytes 8192 | tf_op jit(solution)/shard_map/all_to_all | solution.py:105
  200.2 4.4 %copy-start.4 = (f32[1280]{0:T(1024)S(1)}, f32[1280]{0:T(1024)}, u32[]{:S(2)}) copy-start(f32[1280]{0:T(1024)} %param.12) | copy-start | bytes 15364
  207.5 37.2 %all-to-all-start.2 = ((bf16[16,8,5120]{2,0,1:T(8,128)(2,1)}), bf16[16,8,5120]{2,0,1:T(8,128)(2,1)S(1)}, u32[]{:S(2)}, u32[]{:S(2)}) async-start(bf16[16,8,5120]{2,0,1:T(8,128)(2,1)} %copy.48), calls=%async_computation.2 | async-start | bytes 2621440 | tf_op jit(solution)/shard_map/all_to_all | solution.py:104
Sparse Core Ops, SparseCore 0:
  9.5 57.1 all-gather.3
  71.2 85.0 all-gather.5
